TPU v7x, 512 devices: a whole 4x4x16 slice. The times are simulated.
512 devices in a mesh: ep: 128 (over x, z, core), rep: 4 (over y).
Axes of the slice: x: 4, y: 4, z: 16, core: 2. Of those that a mesh axis runs over, the one named last changes fastest.
Arguments:
- tension: float32 [65536, 512], P(('rep', 'ep')), parts along dimension 0, may hold values from -6 to 6
- tile_dest: int32 [65536], P(('rep', 'ep')), parts along dimension 0, may hold values from 0 to 16383, as said below
- restriction: float32 [8, 64], replicated, may hold values from -0.75 to 0.75
- elem_block: int32 [524288], P(('rep', 'ep')), parts along dimension 0, may hold values from 0 to 1023
- shared_own: int32 [131072], P(('rep', 'ep')), parts along dimension 0, may hold values from 0 to 1023, as said below
- shared_send: int32 [131072], P(('rep', 'ep')), parts along dimension 0, may hold values from 0 to 1023
Outputs:
- quadrature: float32 [8, 524288], P(None, ('rep', 'ep')), parts along dimension 1
There are 4 independent parts, one for each index of `rep`. A program takes and returns all parts, laid end to end along the dimension named above; an argument that names none is the same for every part. Nothing has to cross between parts.
Inputs may be any that keep to these rules, and one draw needn't show every extreme that they name: `tile_dest`: A permutation of the tile positions. The 128 entries of one device name, for each device's block of 128 positions, either exactly 2 positions in it or none. `shared_own`: the 256 entries of one device are distinct.
All inputs are finite; a program needn't handle non-finite values.
Results may differ from a plain program's by a relative error of at most 0.00007.
Values sent between devices are 32-bit elements; how exact they have to be, the bound alone decides.
No kernel may reach another device: no remote copies, remote signals or barrier semaphores. Data moves between devices by JAX's collectives and lax.ppermute only.
A program may use at most 64 MiB of HBM per device.

v0:
```python
import jax
import jax.numpy as jnp
from jax import lax
from jax.sharding import PartitionSpec as P

ELEM_NODES = 64


def from_behind(array, axis, by):
    length = lax.axis_size(axis)
    return lax.ppermute(array, axis, [(i, (i + by) % length) for i in range(length)])


def per_device(tension, tile_dest, restriction, elem_block, shared_own, shared_send):
    tile_dev = tension.shape[0]
    peer_count = lax.axis_size("ep")
    capacity = 2 * tile_dev // peer_count
    target = tile_dest // tile_dev
    onehot = (target[:, None] == jnp.arange(peer_count, dtype=jnp.int32)[None, :]).astype(jnp.int32)
    before = jnp.cumsum(onehot, axis=0) - onehot
    send_rank = jnp.sum(before * onehot, axis=1)
    send_slot = target * capacity + send_rank
    where_to = (
        jnp.full((peer_count * capacity,), tile_dev, jnp.int32)
        .at[send_slot]
        .set(tile_dest % tile_dev)
    )
    where_to = where_to.reshape(peer_count, capacity)
    local_quad = jnp.dot(
        tension.reshape(-1, ELEM_NODES),
        restriction.T,
        precision=lax.Precision.HIGHEST,
        preferred_element_type=jnp.float32,
    )
    local_quad = local_quad.reshape(tile_dev, -1)
    row_width = local_quad.shape[1]
    outbox = (
        jnp.zeros((peer_count * capacity, row_width), jnp.float32).at[send_slot].set(local_quad)
    )
    inbox, arrivals = (
        lax.all_to_all(
            outbox.reshape(peer_count, capacity, row_width),
            "ep",
            split_axis=0,
            concat_axis=0,
            tiled=True,
        ),
        lax.all_to_all(where_to, "ep", split_axis=0, concat_axis=0, tiled=True),
    )
    placed = (
        jnp.zeros((tile_dev, row_width), jnp.float32)
        .at[arrivals.reshape(-1)]
        .set(inbox.reshape(peer_count * capacity, row_width), mode="drop")
    )
    quad_values = placed.reshape(-1, restriction.shape[0])[elem_block]
    outgoing = quad_values[shared_send]
    incoming = from_behind(outgoing, "ep", -1)
    mixed = 0.5 * (quad_values[shared_own] + incoming)
    averaged = quad_values.at[shared_own].set(mixed)
    return averaged.T


def solution(mesh):
    return jax.shard_map(
        per_device,
        mesh=mesh,
        in_specs=(
            P(("rep", "ep"), None),
            P(("rep", "ep")),
            P(),
            P(("rep", "ep")),
            P(("rep", "ep")),
            P(("rep", "ep")),
        ),
        out_specs=P(None, ("rep", "ep")),
        check_vma=False,
    )
```

profile of v0, /device:TPU:1, one launch (start us, length us, event | category | flops | bytes accessed | tf_op | source)
XLA Modules:
  0.0 75.7 jit_solution(11204769958460519604)
XLA Ops:
  0.0 0.0 copy-start
  0.0 0.0 copy-start.1
  0.0 0.7 and_select_fusion
  0.7 0.1 fusion.6
  0.8 0.2 reduce_window_sum.11
  1.0 0.2 select_reduce_fusion
  1.2 1.0 %scatter_custom_fusion = s32[256]{0:T(256)S(1)} fusion(s32[128]{0:T(128)S(1)} %compare_select_fusion.4, s32[128]{0:T(128)S(1)} %get-tuple-element.5, s32[]{:T(128)} %constant.39.clone.1), kind=kCustom, calls=%fused_computation.31 | custom fusion | bytes 1028 | tf_op jit(solution)/shard_map/scatter | solution.py:26
  2.2 0.8 %all_to_all.9 = s32[128,1,2]{2,0,1:T(8,128)} reshape(s32[256]{0:T(256)S(1)} %scatter_custom_fusion) | data formatting | bytes 2048 | tf_op jit(solution)/shard_map/all_to_all | solution.py:48
  2.9 0.0 copy-start.3
  2.9 0.0 copy-start.2
  2.9 20.5 %all-to-all-start = ((s32[128,1,2]{2,1,0:T(1,128)}), s32[128,1,2]{2,1,0:T(1,128)S(1)}, u32[]{:S(2)}, u32[]{:S(2)}) async-start(s32[128,1,2]{2,1,0:T(1,128)} %bitcast), calls=%async_computation | async-start | bytes 131072 | tf_op jit(solution)/shard_map/all_to_all | solution.py:48
  23.4 0.0 copy-done.3
  23.5 0.0 copy-done.2
  23.5 0.0 copy-done.1
  23.5 0.1 reshape.53
  23.6 0.0 copy-done
  23.6 0.0 copy-start.4
  23.7 0.5 fusion.13
  24.2 0.1 copy-done.4
  24.3 0.2 reshape.94
  24.5 0.9 %scatter_custom_fusion.1 = f32[256,64]{1,0:T(8,128)S(1)} fusion(s32[128]{0:T(128)S(1)} %compare_select_fusion.4, f32[128,64]{1,0:T(8,128)S(1)} %reshape.94, f32[]{:T(128)} %constant.38.clone.1), kind=kCustom, calls=%fused_computation.11 | custom fusion | bytes 65540 | tf_op jit(solution)/shard_map/scatter | solution.py:38
  25.4 0.8 %reshape.145 = f32[128,1,128]{2,1,0:T(1,128)} reshape(f32[128,2,64]{2,1,0:T(2,128)S(1)} %bitcast.12) | data formatting | bytes 131072
  26.2 12.3 %all-to-all-done = s32[128,1,2]{2,1,0:T(1,128)S(1)} async-done(((s32[128,1,2]{2,1,0:T(1,128)}), s32[128,1,2]{2,1,0:T(1,128)S(1)}, u32[]{:S(2)}, u32[]{:S(2)}) %all-to-all-start) | async-done | bytes 1056 | tf_op jit(solution)/shard_map/all_to_all | solution.py:48
  38.5 6.6 %all-to-all-start.1 = ((f32[128,1,128]{2,1,0:T(1,128)}), f32[128,1,128]{2,1,0:T(1,128)S(1)}, u32[]{:S(2)}, u32[]{:S(2)}) async-start(f32[128,1,128]{2,1,0:T(1,128)} %reshape.145), calls=%async_computation.1 | async-start | bytes 131072 | tf_op jit(solution)/shard_map/all_to_all | solution.py:41
  45.0 0.5 broadcast.92
  45.5 0.8 %reduce.3 = s32[128,2]{1,0:T(8,128)S(1)} reduce(s32[128,1,2]{2,1,0:T(1,128)S(1)} %all-to-all-done, s32[]{:T(128)} %broadcast.92), dimensions={1}, to_apply=%all_to_all.10.reduce_sub_computation.3 | reduce | bytes 2052 | tf_op jit(solution)/shard_map/all_to_all | solution.py:48
  46.4 0.1 reshape.52
  46.5 13.6 %all-to-all-done.1 = f32[128,1,128]{2,1,0:T(1,128)S(1)} async-done(((f32[128,1,128]{2,1,0:T(1,128)}), f32[128,1,128]{2,1,0:T(1,128)S(1)}, u32[]{:S(2)}, u32[]{:S(2)}) %all-to-all-start.1) | async-done | bytes 65568 | tf_op jit(solution)/shard_map/all_to_all | solution.py:41
  60.1 0.5 broadcast.93
  60.7 0.8 %reduce.4 = f32[128,128]{1,0:T(8,128)S(1)} reduce(f32[128,1,128]{2,1,0:T(1,128)S(1)} %all-to-all-done.1, f32[]{:T(128)} %broadcast.93), dimensions={1}, to_apply=%all_to_all.11.reduce_sub_computation | reduce | bytes 131076 | tf_op jit(solution)/shard_map/all_to_all | solution.py:41
  61.5 0.1 reshape.146
  61.6 1.2 %scatter_custom_fusion.2 = f32[128,64]{1,0:T(8,128)S(1)} fusion(s32[256]{0:T(256)S(1)} %bitcast.14, f32[256,64]{1,0:T(8,128)S(1)} %bitcast.13, f32[]{:T(128)} %constant.38.clone.1), kind=kCustom, calls=%fused_computation.16 | custom fusion | bytes 32772 | tf_op jit(solution)/shard_map/scatter | solution.py:53
  62.8 0.2 reshape.57
  63.0 2.8 %gather_fusion = f32[1024,8]{1,0:T(8,128)S(1)} fusion(f32[1024,8]{1,0:T(8,128)S(1)} %reshape.57, s32[1024]{0:T(1024)S(1)} %fusion.9), kind=kCustom, calls=%fused_computation | custom fusion | bytes 69632 | tf_op jit(solution)/shard_map/gather | solution.py:55
  65.8 0.7 gather_fusion.1
  66.5 3.3 %collective-permute-start = (f32[256,8]{1,0:T(8,128)S(1)}, f32[256,8]{1,0:T(8,128)S(1)}, u32[]{:S(2)}, u32[]{:S(2)}) collective-permute-start(f32[256,8]{1,0:T(8,128)S(1)} %gather_fusion.1), channel_id=1, source_target_pairs={{0,508},{4,0},{8,4},{12,8},{16,12},{20,16},{24,20},{28,24},{32,28}... | collective-permute-start | bytes 24584 | tf_op jit(solution)/shard_map/ppermute | solution.py:11
  69.9 2.9 %collective-permute-done = f32[256,8]{1,0:T(8,128)S(1)} collective-permute-done((f32[256,8]{1,0:T(8,128)S(1)}, f32[256,8]{1,0:T(8,128)S(1)}, u32[]{:S(2)}, u32[]{:S(2)}) %collective-permute-start) | collective-permute-done | bytes 8224 | tf_op jit(solution)/shard_map/ppermute | solution.py:11
  72.8 2.1 %scatter_custom_fusion.3 = f32[1024,8]{1,0:T(8,128)S(1)} fusion(f32[1024,8]{1,0:T(8,128)S(1)} %gather_fusion, s32[256]{0:T(256)S(1)} %compare_select_fusion.3, f32[256,8]{1,0:T(8,128)S(1)} %collective-permute-done, f32[]{:T(128)} %constant.48.clone.1, s32[1024]{0:T(1024)S(1)} %pad_clamp_fusion.1), kind=kCustom, calls=%fused_computation.7 | custom fusion | flops 4096 | bytes 692228 | tf_op jit(solution)/shard_map/scatter | solution.py:59
  74.9 0.8 %copy.12 = f32[8,1024]{1,0:T(8,128)} copy(f32[8,1024]{0,1:T(8,128)S(1)} %bitcast.11) | data formatting | bytes 65536 | tf_op jit(solution)/shard_map/transpose | solution.py:60
  (7 shorter events, 0.0 us)
Async XLA Ops:
  0.0 23.6 %copy-start = (f32[8,64]{1,0:T(8,128)S(1)}, f32[8,64]{1,0:T(8,128)}, u32[]{:S(2)}) copy-start(f32[8,64]{1,0:T(8,128)} %param.8) | copy-start | bytes 6148
  0.0 23.5 %copy-start.1 = (f32[128,512]{1,0:T(8,128)S(1)}, f32[128,512]{1,0:T(8,128)}, u32[]{:S(2)}) copy-start(f32[128,512]{1,0:T(8,128)} %param.6) | copy-start | bytes 786436
  2.9 20.5 %copy-start.3 = (s32[256]{0:T(256)S(1)}, s32[256]{0:T(256)}, u32[]{:S(2)}) copy-start(s32[256]{0:T(256)} %param.10) | copy-start | bytes 3076
  2.9 20.5 %copy-start.2 = (s32[1024]{0:T(1024)S(1)}, s32[1024]{0:T(1024)}, u32[]{:S(2)}) copy-start(s32[1024]{0:T(1024)} %param.9) | copy-start | bytes 12292
  2.9 35.5 %all-to-all-start = ((s32[128,1,2]{2,1,0:T(1,128)}), s32[128,1,2]{2,1,0:T(1,128)S(1)}, u32[]{:S(2)}, u32[]{:S(2)}) async-start(s32[128,1,2]{2,1,0:T(1,128)} %bitcast), calls=%async_computation | async-start | bytes 131072 | tf_op jit(solution)/shard_map/all_to_all | solution.py:48
  23.6 0.7 copy-start.4
  38.5 21.7 %all-to-all-start.1 = ((f32[128,1,128]{2,1,0:T(1,128)}), f32[128,1,128]{2,1,0:T(1,128)S(1)}, u32[]{:S(2)}, u32[]{:S(2)}) async-start(f32[128,1,128]{2,1,0:T(1,128)} %reshape.145), calls=%async_computation.1 | async-start | bytes 131072 | tf_op jit(solution)/shard_map/all_to_all | solution.py:41
  66.5 6.3 %collective-permute-start = (f32[256,8]{1,0:T(8,128)S(1)}, f32[256,8]{1,0:T(8,128)S(1)}, u32[]{:S(2)}, u32[]{:S(2)}) collective-permute-start(f32[256,8]{1,0:T(8,128)S(1)} %gather_fusion.1), channel_id=1, source_target_pairs={{0,508},{4,0},{8,4},{12,8},{16,12},{20,16},{24,20},{28,24},{32,28}... | collective-permute-start | bytes 24584 | tf_op jit(solution)/shard_map/ppermute | solution.py:11
where the time goes:
time: 76 us; the launch traced here: 75.7 us
  starting transfers between devices  30.4 us (40%)
  waiting for transfers between devices  28.8 us (38%)
  local copies, waits for them, and re-layouts  10.8 us (14%)
  other arithmetic  4.91 us (6%)
    all_to_all x1, starting transfers between devices, per_device(): lax.all_to_all(where_to, 'ep', split_axis=0, concat_axis=0, tiled=True)  20.5 us
    all_to_all x1, waiting for transfers between devices, per_device(): lax.all_to_all(outbox.reshape(peer_count, capacity, row_width), 'ep', spl...  13.6 us
    all_to_all x1, waiting for transfers between devices, per_device(): lax.all_to_all(where_to, 'ep', split_axis=0, concat_axis=0, tiled=True)  12.3 us
    all_to_all x1, starting transfers between devices, per_device(): lax.all_to_all(outbox.reshape(peer_count, capacity, row_width), 'ep', spl...  6.56 us
    ppermute x1, starting transfers between devices, from_behind(): lax.ppermute(array, axis, [(i, (i + by) % length) for i in range(length)])  3.35 us
    ppermute x1, waiting for transfers between devices, from_behind(): lax.ppermute(array, axis, [(i, (i + by) % length) for i in range(length)])  2.92 us
    gather x1, local copies, waits for them, and re-layouts, per_device(): quad_values = placed.reshape(-1, restriction.shape[0])[elem_block]  2.81 us
    scatter x1, other arithmetic, per_device(): averaged = quad_values.at[shared_own].set(mixed)  2.12 us
  transfers between devices with their start and end apart: 3, of which 3 were waited for; matrix products, arithmetic and copies ran while one was open for 5% of the time, Pallas kernels for 0%

commit v1 on v0

v1 whole, which is shorter than its diff:
```python
import jax
import jax.numpy as jnp
from jax import lax
from jax.experimental import pallas as pl
from jax.experimental.pallas import tpu as pltpu
from jax.sharding import Mesh
from jax.sharding import PartitionSpec as P

LANES = 128
TILE_DEV = 128
ELEM_DEV = 1024
SHARED = 256
BLOCKS = 8
QUAD = 8
WIDTH = BLOCKS * QUAD
CHIPS = 64
ROWS = 4


def iota(shape, dim):
    return lax.broadcasted_iota(jnp.int32, shape, dim)


def split3(x):
    high = x.astype(jnp.bfloat16)
    rest = x - high.astype(jnp.float32)
    mid = rest.astype(jnp.bfloat16)
    low = (rest - mid.astype(jnp.float32)).astype(jnp.bfloat16)
    return high, mid, low


def dot(a, b, contract, **kw):
    return lax.dot_general(a, b, ((contract[:1], contract[1:]), ((), ())), preferred_element_type=jnp.float32, **kw)


def pack_kernel(tension_ref, dest_ref, restriction_ref, out_ref):
    wide = jnp.concatenate([restriction_ref[...]] * BLOCKS, axis=1)
    block = iota(wide.shape, 1) // (wide.shape[1] // BLOCKS)
    weight = jnp.concatenate([jnp.where(block == b, wide, 0.0) for b in range(BLOCKS)], axis=0)
    quad = dot(tension_ref[...], weight, (1, 1), precision=lax.Precision.HIGHEST)
    dest = dest_ref[...]
    target = dest // TILE_DEV
    position = (dest % TILE_DEV).astype(jnp.float32)
    shape = (2 * CHIPS, TILE_DEV)
    row, lane = iota(shape, 0), iota(shape, 1)
    owner = jnp.where(row < CHIPS, 2 * row, 2 * row - (2 * CHIPS - 1))
    hit = jnp.broadcast_to(target, shape) == owner
    lane_f = lane.astype(jnp.float32)
    first = jnp.min(jnp.where(hit, lane_f, float(TILE_DEV)), axis=1, keepdims=True)
    one = lane_f == first
    two = jnp.logical_and(hit, lane_f != first)
    spread = jnp.broadcast_to(position, shape)
    where_one = jnp.max(jnp.where(one, spread, -1.0), axis=1, keepdims=True)
    where_two = jnp.max(jnp.where(two, spread, -1.0), axis=1, keepdims=True)
    pick = jnp.concatenate(
        [jnp.where(one, 1.0, 0.0).astype(jnp.bfloat16), jnp.where(two, 1.0, 0.0).astype(jnp.bfloat16)], axis=1
    )
    data = jnp.zeros(shape, jnp.float32)
    for part in split3(quad):
        nil = jnp.zeros_like(part)
        both = jnp.concatenate(
            [jnp.concatenate([part, nil], axis=1), jnp.concatenate([nil, part], axis=1)], axis=0
        )
        data = data + dot(pick, both, (1, 0))
    even, odd = data[:CHIPS], data[CHIPS:]

    def ahead(x):
        return jnp.concatenate([x[1:], x[:1]], axis=0)

    column = lane[:CHIPS]
    places = jnp.zeros((CHIPS, LANES), jnp.float32)
    firsts, seconds = where_one[:CHIPS], where_two[:CHIPS]
    columns = (firsts, seconds, where_one[CHIPS:], where_two[CHIPS:], ahead(firsts), ahead(seconds))
    for i, value in enumerate(columns):
        places = jnp.where(column == i, jnp.broadcast_to(value, places.shape), places)
    for i, value in enumerate((even, odd, ahead(even), places)):
        out_ref[pl.ds(i, CHIPS, stride=ROWS), :] = value


def send_index_kernel(block_ref, send_ref, _, out_ref):
    block = block_ref[...]
    row = iota((QUAD, ELEM_DEV), 0)
    wide = jnp.broadcast_to(block, row.shape)
    left = jnp.where(row == 0, wide // BLOCKS, jnp.where(row == 1, wide % BLOCKS, 0))
    shape = (ELEM_DEV, SHARED)
    pick = jnp.where(iota(shape, 0) == jnp.broadcast_to(send_ref[...], shape), 1.0, 0.0)
    out_ref[...] = dot(left.astype(jnp.float32).astype(jnp.bfloat16), pick.astype(jnp.bfloat16), (1, 0))


def own_index_kernel(index_ref, own_ref, out_ref):
    index = index_ref[...]
    row = iota(index.shape, 0)
    left = jnp.where(row == 2, 1.0, index)
    shape = (ELEM_DEV, SHARED)
    pick = jnp.where(iota(shape, 0) == jnp.broadcast_to(own_ref[...], shape), 1.0, 0.0)
    placed = dot(left.astype(jnp.bfloat16), pick.astype(jnp.bfloat16), (1, 1))
    shared = placed[2:3] > 0.5
    out_ref[...] = jnp.where(iota(placed.shape, 0) == 0, jnp.where(shared, placed, -1.0), placed)


def gather(table, places, tile, block):
    turned = table.T
    left = jnp.concatenate(
        [jnp.concatenate([part[:WIDTH], part[WIDTH:]], axis=1) for part in split3(turned)], axis=0
    )
    shape = (TILE_DEV, tile.shape[1])
    wide = jnp.broadcast_to(tile, shape)
    pick = jnp.concatenate(
        [jnp.where(jnp.broadcast_to(place, shape) == wide, 1.0, 0.0).astype(jnp.bfloat16) for place in places], axis=0
    )
    tall = dot(left, pick, (1, 0))
    tall = tall[:WIDTH] + tall[WIDTH : 2 * WIDTH] + tall[2 * WIDTH :]
    which = jnp.broadcast_to(block, (QUAD, tile.shape[1]))
    out = jnp.zeros(which.shape, jnp.float32)
    for b in range(BLOCKS):
        out = jnp.where(which == float(b), tall[b * QUAD : (b + 1) * QUAD], out)
    return out


def place_kernel(core_ref, inbox_ref, block_ref, ghost_ref, out_ref):
    even_core = core_ref[0] == 0
    rows = [inbox_ref[pl.ds(i, 2 * CHIPS, stride=ROWS), :] for i in range(ROWS)]
    own = jnp.where(even_core, rows[0], rows[1])
    following = jnp.where(even_core, rows[1], rows[2])
    places = jnp.where(even_core, rows[3], pltpu.roll(rows[3], LANES - 2, 1))
    block = block_ref[...]
    mine = gather(
        own,
        (places[:, 0:1], places[:, 1:2]),
        (block // BLOCKS).astype(jnp.float32),
        (block % BLOCKS).astype(jnp.float32),
    )
    tile = ghost_ref[0:1, :]
    ghost = gather(following, (places[:, 2:3], places[:, 3:4]), tile, ghost_ref[1:2, :])
    shared = jnp.broadcast_to(tile, ghost.shape) >= 0.0
    out_ref[...] = jnp.where(shared, 0.5 * (mine + ghost), mine)


def call(kernel, shape, scalar=False):
    kw = {}
    return pl.pallas_call(
        kernel,
        out_shape=jax.ShapeDtypeStruct(shape, jnp.float32),
        name=kernel.__name__,
        **kw,
    )


def per_device(tension, tile_dest, restriction, elem_block, shared_own, shared_send):
    core = lax.axis_index("core").reshape(1)
    outbox = call(pack_kernel, (CHIPS * ROWS, LANES))(tension, tile_dest.reshape(1, -1), restriction)
    inbox = lax.all_to_all(outbox.reshape(CHIPS, ROWS, LANES), "chip", 0, 0, tiled=True)
    index = call(send_index_kernel, (QUAD, SHARED))(
        elem_block.reshape(1, -1), shared_send.reshape(1, -1), outbox[:8]
    )
    count = 2 * CHIPS
    index = lax.ppermute(index, ("chip", "core"), [(i, (i - 1) % count) for i in range(count)])
    ghost = call(own_index_kernel, (QUAD, ELEM_DEV))(index, shared_own.reshape(1, -1))
    inbox = lax.all_gather(inbox.reshape(CHIPS * ROWS, LANES), "core", tiled=True)
    return pl.pallas_call(
        place_kernel,
        out_shape=jax.ShapeDtypeStruct((QUAD, ELEM_DEV), jnp.float32),
        in_specs=[pl.BlockSpec(memory_space=pltpu.SMEM)] + [pl.BlockSpec(memory_space=pltpu.VMEM)] * 3,
        name="place_kernel",
    )(core, inbox, elem_block.reshape(1, -1), ghost)


def solution(mesh):
    split = Mesh(mesh.devices.reshape(CHIPS, 2, -1), ("chip", "core", "rep"))
    spread = P(("rep", "chip", "core"))
    return jax.shard_map(
        per_device,
        mesh=split,
        in_specs=(spread, spread, P(), spread, spread, spread),
        out_specs=P(None, ("rep", "chip", "core")),
        check_vma=False,
    )
```

time: 76 us -> 43 us (0.57)
  waiting for transfers between devices: 28.8 us -> 6.45 us
  local copies, waits for them, and re-layouts: 10.8 us -> 1.86 us
  starting transfers between devices: 30.4 us -> 21.9 us
  Pallas kernels: 0 us -> 7.66 us
  other arithmetic: 4.91 us -> 0 us
  blocking collectives: 0 us -> 4.75 us
    all_to_all x2 -> x1, waiting for transfers between devices: 25.9 us -> 3.39 us  [per_device(): lax.all_to_all(outbox.reshape(CHIPS, ROWS, LANES), 'chip', 0, 0, tiled=True)]
    all_to_all x2 -> x1, starting transfers between devices: 27.1 us -> 19.1 us  [per_device(): lax.all_to_all(outbox.reshape(CHIPS, ROWS, LANES), 'chip', 0, 0, tiled=True)]
    pallas_call x0 -> x4, Pallas kernels: none -> 7.66 us  [the longest x1 2.39 us: per_device(): call(pack_kernel, (CHIPS * ROWS, LANES))]
    all_gather x0 -> x1, blocking collectives: none -> 4.75 us  [per_device(): lax.all_gather(inbox.reshape(CHIPS * ROWS, LANES), 'core', tiled=True)]
    gather x2 -> x0, local copies, waits for them, and re-layouts: 3.54 us -> none  [the longest x1 2.81 us: per_device(): quad_values = placed.reshape(-1, restriction.shape[0])[elem_block]]
    scatter x3 -> x0, local copies, waits for them, and re-layouts: 3.06 us -> none  [the longest x1 1.17 us: per_device(): placed = jnp.zeros((tile_dev, row_width), jnp.float32).at[arrivals.reshap...]
    scatter x1 -> x0, other arithmetic: 2.12 us -> none  [per_device(): averaged = quad_values.at[shared_own].set(mixed)]
    all_to_all x3 -> x0, local copies, waits for them, and re-layouts: 1.78 us -> none  [the longest x2 1.27 us: per_device(): lax.all_to_all(where_to, 'ep', split_axis=0, concat_axis=0, tiled=True)]
  transfers between devices with their start and end apart: 3 -> 2, of which waited for: 3 -> 2; matrix products, arithmetic and copies ran while one was open for 5% -> 3% of each run, Pallas kernels for 0% -> 7%
where the time goes in v1:
time: 43 us; the launch traced here: 42.7 us
  starting transfers between devices  21.9 us (51%)
  Pallas kernels  7.66 us (18%)
  waiting for transfers between devices  6.45 us (15%)
  blocking collectives  4.75 us (11%)
  local copies, waits for them, and re-layouts  1.86 us (4%)
    all_to_all x1, starting transfers between devices, per_device(): lax.all_to_all(outbox.reshape(CHIPS, ROWS, LANES), 'chip', 0, 0, tiled=True)  19.1 us
    all_gather x1, blocking collectives, per_device(): lax.all_gather(inbox.reshape(CHIPS * ROWS, LANES), 'core', tiled=True)  4.75 us
    all_to_all x1, waiting for transfers between devices, per_device(): lax.all_to_all(outbox.reshape(CHIPS, ROWS, LANES), 'chip', 0, 0, tiled=True)  3.39 us
    ppermute x1, waiting for transfers between devices, per_device(): lax.ppermute(index, ('chip', 'core'), [(i, (i - 1) % count) for i in rang...  3.06 us
    ppermute x1, starting transfers between devices, per_device(): lax.ppermute(index, ('chip', 'core'), [(i, (i - 1) % count) for i in rang...  2.85 us
    pallas_call x1, Pallas kernels, per_device(): call(pack_kernel, (CHIPS * ROWS, LANES))  2.39 us
    pallas_call x1, Pallas kernels, per_device(): pl.pallas_call(place_kernel, out_shape=jax.ShapeDtypeStruct((QUAD, ELEM_D...  2.16 us
    pallas_call x1, Pallas kernels, per_device(): call(own_index_kernel, (QUAD, ELEM_DEV))(index, shared_own.reshape(1, -1))  1.57 us
  transfers between devices with their start and end apart: 2, of which 2 were waited for; matrix products, arithmetic and copies ran while one was open for 3% of the time, Pallas kernels for 7%

profile of v1, /device:TPU:1, one launch (start us, length us, event | category | flops | bytes accessed | tf_op | source)
XLA Modules:
  0.0 42.7 jit_solution(17242271798251736108)
XLA Ops:
  0.0 2.4 %pack_kernel.1 = f32[256,128]{1,0:T(8,128)} custom-call(f32[128,512]{1,0:T(8,128)} %tension_ref.1, s32[1,128]{1,0:T(1,128)} %bitcast.13, f32[8,64]{1,0:T(8,128)} %restriction_ref.1), custom_call_target="tpu_custom_call" | custom-call | tf_op jit(solution)/shard_map/pack_kernel/pallas_call | solution.py:151
  2.4 19.1 %all-to-all-start = ((f32[64,4,128]{2,1,0:T(4,128)}), f32[64,4,128]{2,1,0:T(4,128)S(1)}, u32[]{:S(2)}, u32[]{:S(2)}) async-start(f32[64,4,128]{2,1,0:T(4,128)} %bitcast.7), calls=%async_computation | async-start | bytes 262144 | tf_op jit(solution)/shard_map/all_to_all | solution.py:152
  21.5 1.3 %slice.4._ = f32[8,128]{1,0:T(8,128)} slice(f32[256,128]{1,0:T(8,128)} %pack_kernel.1), slice={[0:8], [0:128]} | slice | bytes 8192 | tf_op jit(solution)/shard_map/slice | solution.py:154
  22.8 1.5 %send_index_kernel.1 = f32[8,256]{1,0:T(8,128)} custom-call(s32[1,1024]{1,0:T(1,128)} %bitcast.9, s32[1,256]{1,0:T(1,128)} %bitcast.11, f32[8,128]{1,0:T(8,128)} %slice.4._), custom_call_target="tpu_custom_call" | custom-call | tf_op jit(solution)/shard_map/send_index_kernel/pallas_call | solution.py:153
  24.3 2.8 %collective-permute-start = (f32[8,256]{1,0:T(8,128)}, f32[8,256]{1,0:T(8,128)S(1)}, u32[]{:S(2)}, u32[]{:S(2)}) collective-permute-start(f32[8,256]{1,0:T(8,128)} %send_index_kernel.1), channel_id=1, source_target_pairs={{0,508},{4,0},{8,4},{12,8},{16,12},{20,16},{24,20},{28,24},{32,28}... | collective-permute-start | bytes 24584 | tf_op jit(solution)/shard_map/ppermute | solution.py:157
  27.2 3.1 %collective-permute-done.index_ref = f32[8,256]{1,0:T(8,128)S(1)} collective-permute-done((f32[8,256]{1,0:T(8,128)}, f32[8,256]{1,0:T(8,128)S(1)}, u32[]{:S(2)}, u32[]{:S(2)}) %collective-permute-start) | collective-permute-done | bytes 8224 | tf_op jit(solution)/shard_map/ppermute | solution.py:157
  30.2 0.0 copy-start
  30.2 0.6 %copy-done = f32[8,256]{1,0:T(8,128)} copy-done((f32[8,256]{1,0:T(8,128)}, f32[8,256]{1,0:T(8,128)S(1)}, u32[]{:S(2)}) %copy-start) | copy-done | bytes 8216
  30.8 1.6 %own_index_kernel.1.ghost_ref = f32[8,1024]{1,0:T(8,128)} custom-call(f32[8,256]{1,0:T(8,128)} %copy-done, s32[1,256]{1,0:T(1,128)} %bitcast.12), custom_call_target="tpu_custom_call" | custom-call | tf_op jit(solution)/shard_map/own_index_kernel/pallas_call | solution.py:158
  32.4 3.4 %all-to-all-done = f32[64,4,128]{2,1,0:T(4,128)S(1)} async-done(((f32[64,4,128]{2,1,0:T(4,128)}), f32[64,4,128]{2,1,0:T(4,128)S(1)}, u32[]{:S(2)}, u32[]{:S(2)}) %all-to-all-start) | async-done | bytes 131104 | tf_op jit(solution)/shard_map/all_to_all | solution.py:152
  35.8 4.7 %all_gather.3.inbox_ref = f32[512,128]{1,0:T(8,128)} all-gather(f32[256,128]{1,0:T(8,128)S(1)} %bitcast.8), channel_id=1, replica_groups=mesh['chip'=64,'core'=2,'rep'=4] {'core'}, dimensions={0}, use_global_device_ids=true | all-gather | bytes 393216 | tf_op jit(solution)/shard_map/all_gather | solution.py:159
  40.5 2.2 %place_kernel.1 = f32[8,1024]{1,0:T(8,128)} custom-call(s32[1]{0:T(128)} %bitcast.core_ref, f32[512,128]{1,0:T(8,128)} %all_gather.3.inbox_ref, s32[1,1024]{1,0:T(1,128)} %bitcast.10, f32[8,1024]{1,0:T(8,128)} %own_index_kernel.1.ghost_ref), custom_call_target="tpu_custom_call" | custom-call | tf_op jit(solution)/shard_map/place_kernel/pallas_call | solution.py:160
Async XLA Ops:
  2.4 33.4 %all-to-all-start = ((f32[64,4,128]{2,1,0:T(4,128)}), f32[64,4,128]{2,1,0:T(4,128)S(1)}, u32[]{:S(2)}, u32[]{:S(2)}) async-start(f32[64,4,128]{2,1,0:T(4,128)} %bitcast.7), calls=%async_computation | async-start | bytes 262144 | tf_op jit(solution)/shard_map/all_to_all | solution.py:152
  24.3 5.9 %collective-permute-start = (f32[8,256]{1,0:T(8,128)}, f32[8,256]{1,0:T(8,128)S(1)}, u32[]{:S(2)}, u32[]{:S(2)}) collective-permute-start(f32[8,256]{1,0:T(8,128)} %send_index_kernel.1), channel_id=1, source_target_pairs={{0,508},{4,0},{8,4},{12,8},{16,12},{20,16},{24,20},{28,24},{32,28}... | collective-permute-start | bytes 24584 | tf_op jit(solution)/shard_map/ppermute | solution.py:157
  30.2 0.6 %copy-start = (f32[8,256]{1,0:T(8,128)}, f32[8,256]{1,0:T(8,128)S(1)}, u32[]{:S(2)}) copy-start(f32[8,256]{1,0:T(8,128)S(1)} %collective-permute-done.index_ref) | copy-start | bytes 24580

commit v2 on v1

--- a/solution.py
+++ b/solution.py
@@ -33,14 +33,19 @@
     return lax.dot_general(a, b, ((contract[:1], contract[1:]), ((), ())), preferred_element_type=jnp.float32, **kw)
 
 
-def pack_kernel(tension_ref, dest_ref, restriction_ref, out_ref):
+def pack_kernel(tension_any, dest_any, restriction_any, out_ref, token_ref, tension_ref, dest_ref, restriction_ref, sems):
+    pairs = ((restriction_any, restriction_ref), (dest_any, dest_ref), (tension_any, tension_ref))
+    copies = [pltpu.make_async_copy(a, b, sems.at[i]) for i, (a, b) in enumerate(pairs)]
+    for copy in copies:
+        copy.start()
+    copies[0].wait()
     wide = jnp.concatenate([restriction_ref[...]] * BLOCKS, axis=1)
     block = iota(wide.shape, 1) // (wide.shape[1] // BLOCKS)
     weight = jnp.concatenate([jnp.where(block == b, wide, 0.0) for b in range(BLOCKS)], axis=0)
-    quad = dot(tension_ref[...], weight, (1, 1), precision=lax.Precision.HIGHEST)
+    copies[1].wait()
     dest = dest_ref[...]
-    target = dest // TILE_DEV
-    position = (dest % TILE_DEV).astype(jnp.float32)
+    target = dest >> 7
+    position = (dest & (TILE_DEV - 1)).astype(jnp.float32)
     shape = (2 * CHIPS, TILE_DEV)
     row, lane = iota(shape, 0), iota(shape, 1)
     owner = jnp.where(row < CHIPS, 2 * row, 2 * row - (2 * CHIPS - 1))
@@ -55,6 +60,8 @@
     pick = jnp.concatenate(
         [jnp.where(one, 1.0, 0.0).astype(jnp.bfloat16), jnp.where(two, 1.0, 0.0).astype(jnp.bfloat16)], axis=1
     )
+    copies[2].wait()
+    quad = dot(tension_ref[...], weight, (1, 1), precision=lax.Precision.HIGHEST)
     data = jnp.zeros(shape, jnp.float32)
     for part in split3(quad):
         nil = jnp.zeros_like(part)
@@ -73,29 +80,37 @@
     columns = (firsts, seconds, where_one[CHIPS:], where_two[CHIPS:], ahead(firsts), ahead(seconds))
     for i, value in enumerate(columns):
         places = jnp.where(column == i, jnp.broadcast_to(value, places.shape), places)
+    token_ref[...] = places[:8]
     for i, value in enumerate((even, odd, ahead(even), places)):
         out_ref[pl.ds(i, CHIPS, stride=ROWS), :] = value
 
 
 def send_index_kernel(block_ref, send_ref, _, out_ref):
     block = block_ref[...]
-    row = iota((QUAD, ELEM_DEV), 0)
-    wide = jnp.broadcast_to(block, row.shape)
-    left = jnp.where(row == 0, wide // BLOCKS, jnp.where(row == 1, wide % BLOCKS, 0))
-    shape = (ELEM_DEV, SHARED)
-    pick = jnp.where(iota(shape, 0) == jnp.broadcast_to(send_ref[...], shape), 1.0, 0.0)
-    out_ref[...] = dot(left.astype(jnp.float32).astype(jnp.bfloat16), pick.astype(jnp.bfloat16), (1, 0))
+    left = jnp.concatenate([block >> 3, block & 7], axis=0).astype(jnp.float32).astype(jnp.bfloat16)
+    send = send_ref[...]
+    shape = (LANES, SHARED)
+    pick = jnp.where(iota(shape, 0) == jnp.broadcast_to(send & (LANES - 1), shape), 1.0, 0.0)
+    rows = dot(left, pick.astype(jnp.bfloat16), (1, 0))
+    shape = (ELEM_DEV // LANES, SHARED)
+    high = iota(shape, 0) == jnp.broadcast_to(send >> 7, shape)
+    tile = jnp.sum(jnp.where(high, rows[: shape[0]], 0.0), axis=0, keepdims=True)
+    block = jnp.sum(jnp.where(high, rows[shape[0] :], 0.0), axis=0, keepdims=True)
+    row = iota((QUAD, SHARED), 0)
+    out_ref[...] = jnp.where(row == 0, jnp.broadcast_to(tile, row.shape), jnp.broadcast_to(block, row.shape))
 
 
-def own_index_kernel(index_ref, own_ref, out_ref):
-    index = index_ref[...]
-    row = iota(index.shape, 0)
-    left = jnp.where(row == 2, 1.0, index)
-    shape = (ELEM_DEV, SHARED)
-    pick = jnp.where(iota(shape, 0) == jnp.broadcast_to(own_ref[...], shape), 1.0, 0.0)
+def own_index_kernel(index_ref, own_ref, tile_ref, block_ref):
+    own = own_ref[...]
+    shape = (ELEM_DEV // LANES, SHARED)
+    high = iota(shape, 0) == jnp.broadcast_to(own >> 7, shape)
+    rows = [index_ref[0:1, :] + 1.0, index_ref[1:2, :]]
+    left = jnp.concatenate([jnp.where(high, jnp.broadcast_to(row, shape), 0.0) for row in rows], axis=0)
+    wide = (LANES, SHARED)
+    pick = jnp.where(iota(wide, 0) == jnp.broadcast_to(own & (LANES - 1), wide), 1.0, 0.0)
     placed = dot(left.astype(jnp.bfloat16), pick.astype(jnp.bfloat16), (1, 1))
-    shared = placed[2:3] > 0.5
-    out_ref[...] = jnp.where(iota(placed.shape, 0) == 0, jnp.where(shared, placed, -1.0), placed)
+    tile_ref[...] = placed[: shape[0]] - 1.0
+    block_ref[...] = placed[shape[0] :]
 
 
 def gather(table, places, tile, block):
@@ -117,7 +132,7 @@
     return out
 
 
-def place_kernel(core_ref, inbox_ref, block_ref, ghost_ref, out_ref):
+def place_kernel(core_ref, inbox_ref, block_ref, tile_ref, ghost_block_ref, out_ref):
     even_core = core_ref[0] == 0
     rows = [inbox_ref[pl.ds(i, 2 * CHIPS, stride=ROWS), :] for i in range(ROWS)]
     own = jnp.where(even_core, rows[0], rows[1])
@@ -127,42 +142,43 @@
     mine = gather(
         own,
         (places[:, 0:1], places[:, 1:2]),
-        (block // BLOCKS).astype(jnp.float32),
-        (block % BLOCKS).astype(jnp.float32),
+        (block >> 3).astype(jnp.float32),
+        (block & 7).astype(jnp.float32),
     )
-    tile = ghost_ref[0:1, :]
-    ghost = gather(following, (places[:, 2:3], places[:, 3:4]), tile, ghost_ref[1:2, :])
+    tile = tile_ref[...]
+    ghost = gather(following, (places[:, 2:3], places[:, 3:4]), tile, ghost_block_ref[...])
     shared = jnp.broadcast_to(tile, ghost.shape) >= 0.0
     out_ref[...] = jnp.where(shared, 0.5 * (mine + ghost), mine)
 
 
-def call(kernel, shape, scalar=False):
-    kw = {}
+def call(kernel, shapes, spaces, scratch=(), limit=4):
     return pl.pallas_call(
         kernel,
-        out_shape=jax.ShapeDtypeStruct(shape, jnp.float32),
+        out_shape=jax.tree.map(lambda s: jax.ShapeDtypeStruct(s, jnp.float32), shapes, is_leaf=lambda s: isinstance(s[0], int)),
+        in_specs=[pl.BlockSpec(memory_space=space) for space in spaces],
+        scratch_shapes=scratch,
+        compiler_params=pltpu.CompilerParams(vmem_limit_bytes=limit << 20),
         name=kernel.__name__,
-        **kw,
     )
 
 
 def per_device(tension, tile_dest, restriction, elem_block, shared_own, shared_send):
+    V, S = pltpu.VMEM, pltpu.SMEM
     core = lax.axis_index("core").reshape(1)
-    outbox = call(pack_kernel, (CHIPS * ROWS, LANES))(tension, tile_dest.reshape(1, -1), restriction)
+    inputs = (tension, tile_dest.reshape(1, -1), restriction)
+    scratch = [V(x.shape, x.dtype) for x in inputs] + [pltpu.SemaphoreType.DMA((3,))]
+    outbox, token = call(pack_kernel, ((CHIPS * ROWS, LANES), (8, LANES)), [pl.ANY] * 3, scratch, 60)(*inputs)
     inbox = lax.all_to_all(outbox.reshape(CHIPS, ROWS, LANES), "chip", 0, 0, tiled=True)
-    index = call(send_index_kernel, (QUAD, SHARED))(
-        elem_block.reshape(1, -1), shared_send.reshape(1, -1), outbox[:8]
+    index = call(send_index_kernel, (QUAD, SHARED), [V, V, V])(
+        elem_block.reshape(-1, LANES), shared_send.reshape(1, -1), token
     )
     count = 2 * CHIPS
     index = lax.ppermute(index, ("chip", "core"), [(i, (i - 1) % count) for i in range(count)])
-    ghost = call(own_index_kernel, (QUAD, ELEM_DEV))(index, shared_own.reshape(1, -1))
+    tile, block = call(own_index_kernel, ((ELEM_DEV // LANES, LANES),) * 2, [V, V])(index, shared_own.reshape(1, -1))
     inbox = lax.all_gather(inbox.reshape(CHIPS * ROWS, LANES), "core", tiled=True)
-    return pl.pallas_call(
-        place_kernel,
-        out_shape=jax.ShapeDtypeStruct((QUAD, ELEM_DEV), jnp.float32),
-        in_specs=[pl.BlockSpec(memory_space=pltpu.SMEM)] + [pl.BlockSpec(memory_space=pltpu.VMEM)] * 3,
-        name="place_kernel",
-    )(core, inbox, elem_block.reshape(1, -1), ghost)
+    return call(place_kernel, (QUAD, ELEM_DEV), [S] + [V] * 4)(
+        core, inbox, elem_block.reshape(1, -1), tile.reshape(1, -1), block.reshape(1, -1)
+    )
 
 
 def solution(mesh):

time: 43 us -> 41.9 us (0.974)
  waiting for transfers between devices: 6.45 us -> 10.4 us
  Pallas kernels: 7.66 us -> 3.83 us
  local copies, waits for them, and re-layouts: 1.86 us -> 0.68 us
    all_to_all x1, waiting for transfers between devices: 3.39 us -> 7.51 us  [per_device(): lax.all_to_all(outbox.reshape(CHIPS, ROWS, LANES), 'chip', 0, 0, tiled=True)]
    pallas_call x4, Pallas kernels: 7.66 us -> 3.83 us  [the longest x1 2.36 us: per_device(): call(pack_kernel, ((CHIPS * ROWS, LANES), (8, LANES)), [pl.ANY] * 3, scra...]
    slice x1 -> x0, local copies, waits for them, and re-layouts: 1.26 us -> none  [per_device(): outbox[:8]]
  transfers between devices with their start and end apart: 2 -> 2, of which waited for: 2 -> 2; matrix products, arithmetic and copies ran while one was open for 3% -> 0% of each run, Pallas kernels for 7% -> 1%
where the time goes in v2:
time: 41.9 us; the launch traced here: 41.6 us
  starting transfers between devices  22 us (53%)
  waiting for transfers between devices  10.4 us (25%)
  blocking collectives  4.62 us (11%)
  Pallas kernels  3.83 us (9%)
  local copies, waits for them, and re-layouts  0.68 us (2%)
    all_to_all x1, starting transfers between devices, per_device(): lax.all_to_all(outbox.reshape(CHIPS, ROWS, LANES), 'chip', 0, 0, tiled=True)  19.1 us
    all_to_all x1, waiting for transfers between devices, per_device(): lax.all_to_all(outbox.reshape(CHIPS, ROWS, LANES), 'chip', 0, 0, tiled=True)  7.51 us
    all_gather x1, blocking collectives, per_device(): lax.all_gather(inbox.reshape(CHIPS * ROWS, LANES), 'core', tiled=True)  4.62 us
    ppermute x1, waiting for transfers between devices, per_device(): lax.ppermute(index, ('chip', 'core'), [(i, (i - 1) % count) for i in rang...  2.91 us
    ppermute x1, starting transfers between devices, per_device(): lax.ppermute(index, ('chip', 'core'), [(i, (i - 1) % count) for i in rang...  2.86 us
    pallas_call x1, Pallas kernels, per_device(): call(pack_kernel, ((CHIPS * ROWS, LANES), (8, LANES)), [pl.ANY] * 3, scra...  2.36 us
    pallas_call x1, Pallas kernels, per_device(): call(place_kernel, (QUAD, ELEM_DEV), [S] + [V] * 4)  1.19 us
  transfers between devices with their start and end apart: 2, of which 2 were waited for; matrix products, arithmetic and copies ran while one was open for 0% of the time, Pallas kernels for 1%

profile of v2, /device:TPU:1, one launch (start us, length us, event | category | flops | bytes accessed | tf_op | source)
XLA Modules:
  0.0 41.6 jit_solution(2585962283238312740)
XLA Ops:
  0.0 2.4 %pack_kernel.1 = (f32[256,128]{1,0:T(8,128)}, f32[8,128]{1,0:T(8,128)}) custom-call(f32[128,512]{1,0:T(8,128)} %tension_any.1, s32[1,128]{1,0:T(1,128)} %bitcast.18, f32[8,64]{1,0:T(8,128)} %restriction_any.1), custom_call_target="tpu_custom_call" | custom-call | tf_op jit(solution)/shard_map/pack_kernel/pallas_call | solution.py:170
  2.4 0.0 copy-start.1
  2.4 19.1 %all-to-all-start = ((f32[64,4,128]{2,1,0:T(4,128)}), f32[64,4,128]{2,1,0:T(4,128)S(1)}, u32[]{:S(2)}, u32[]{:S(2)}) async-start(f32[64,4,128]{2,1,0:T(4,128)} %bitcast.17), calls=%async_computation | async-start | bytes 262144 | tf_op jit(solution)/shard_map/all_to_all | solution.py:171
  21.5 0.0 copy-start
  21.5 0.0 copy-start.2
  21.5 0.0 copy-done.1
  21.5 0.7 %copy-done = s32[1024]{0:T(1024)S(1)} copy-done((s32[1024]{0:T(1024)S(1)}, s32[1024]{0:T(1024)}, u32[]{:S(2)}) %copy-start) | copy-done | bytes 4120
  22.2 0.0 copy-done.2
  22.2 0.1 send_index_kernel.1
  22.3 2.9 %collective-permute-start = (f32[8,256]{1,0:T(8,128)S(1)}, f32[8,256]{1,0:T(8,128)S(1)}, u32[]{:S(2)}, u32[]{:S(2)}) collective-permute-start(f32[8,256]{1,0:T(8,128)S(1)} %send_index_kernel.1), channel_id=1, source_target_pairs={{0,508},{4,0},{8,4},{12,8},{16,12},{20,16},{24,20},{28,24},{32,28}... | collective-permute-start | bytes 24584 | tf_op jit(solution)/shard_map/ppermute | solution.py:176
  25.2 0.0 copy-start.3
  25.2 2.9 %collective-permute-done.index_ref = f32[8,256]{1,0:T(8,128)S(1)} collective-permute-done((f32[8,256]{1,0:T(8,128)S(1)}, f32[8,256]{1,0:T(8,128)S(1)}, u32[]{:S(2)}, u32[]{:S(2)}) %collective-permute-start) | collective-permute-done | bytes 8224 | tf_op jit(solution)/shard_map/ppermute | solution.py:176
  28.1 0.0 copy-done.3
  28.1 0.1 own_index_kernel.1
  28.3 7.5 %all-to-all-done = f32[64,4,128]{2,1,0:T(4,128)S(1)} async-done(((f32[64,4,128]{2,1,0:T(4,128)}), f32[64,4,128]{2,1,0:T(4,128)S(1)}, u32[]{:S(2)}, u32[]{:S(2)}) %all-to-all-start) | async-done | bytes 131104 | tf_op jit(solution)/shard_map/all_to_all | solution.py:171
  35.8 4.6 %all_gather.3.inbox_ref = f32[512,128]{1,0:T(8,128)S(1)} all-gather(f32[256,128]{1,0:T(8,128)S(1)} %bitcast.16), channel_id=1, replica_groups=mesh['chip'=64,'core'=2,'rep'=4] {'core'}, dimensions={0}, use_global_device_ids=true | all-gather | bytes 393216 | tf_op jit(solution)/shard_map/all_gather | solution.py:178
  40.4 1.2 %place_kernel.1 = f32[8,1024]{1,0:T(8,128)} custom-call(s32[1]{0:T(128)} %bitcast.core_ref, f32[512,128]{1,0:T(8,128)S(1)} %all_gather.3.inbox_ref, s32[1,1024]{1,0:T(1,128)S(1)} %bitcast.11, f32[1,1024]{1,0:T(1,128)S(1)} %bitcast.12, f32[1,1024]{1,0:T(1,128)S(1)} %bitcast.13), custom_call_target="tpu_custom_call" | custom-call | tf_op jit(solution)/shard_map/place_kernel/pallas_call | solution.py:179
Async XLA Ops:
  2.4 19.2 %copy-start.1 = (f32[8,128]{1,0:T(8,128)S(1)}, f32[8,128]{1,0:T(8,128)}, u32[]{:S(2)}) copy-start(f32[8,128]{1,0:T(8,128)} %get-tuple-element.10._) | copy-start | bytes 12292
  2.4 33.4 %all-to-all-start = ((f32[64,4,128]{2,1,0:T(4,128)}), f32[64,4,128]{2,1,0:T(4,128)S(1)}, u32[]{:S(2)}, u32[]{:S(2)}) async-start(f32[64,4,128]{2,1,0:T(4,128)} %bitcast.17), calls=%async_computation | async-start | bytes 262144 | tf_op jit(solution)/shard_map/all_to_all | solution.py:171
  21.5 0.7 %copy-start = (s32[1024]{0:T(1024)S(1)}, s32[1024]{0:T(1024)}, u32[]{:S(2)}) copy-start(s32[1024]{0:T(1024)} %param.9) | copy-start | bytes 12292
  21.5 0.7 %copy-start.2 = (s32[256]{0:T(256)S(1)}, s32[256]{0:T(256)}, u32[]{:S(2)}) copy-start(s32[256]{0:T(256)} %param.11) | copy-start | bytes 3076
  22.3 5.8 %collective-permute-start = (f32[8,256]{1,0:T(8,128)S(1)}, f32[8,256]{1,0:T(8,128)S(1)}, u32[]{:S(2)}, u32[]{:S(2)}) collective-permute-start(f32[8,256]{1,0:T(8,128)S(1)} %send_index_kernel.1), channel_id=1, source_target_pairs={{0,508},{4,0},{8,4},{12,8},{16,12},{20,16},{24,20},{28,24},{32,28}... | collective-permute-start | bytes 24584 | tf_op jit(solution)/shard_map/ppermute | solution.py:176
  25.2 2.9 %copy-start.3 = (s32[256]{0:T(256)S(1)}, s32[256]{0:T(256)}, u32[]{:S(2)}) copy-start(s32[256]{0:T(256)} %param.10) | copy-start | bytes 3076

commit v3 on v2

--- a/solution.py
+++ b/solution.py
@@ -15,6 +15,7 @@
 WIDTH = BLOCKS * QUAD
 CHIPS = 64
 ROWS = 4
+FIRST = 42
 
 
 def iota(shape, dim):
@@ -48,7 +49,7 @@
     position = (dest & (TILE_DEV - 1)).astype(jnp.float32)
     shape = (2 * CHIPS, TILE_DEV)
     row, lane = iota(shape, 0), iota(shape, 1)
-    owner = jnp.where(row < CHIPS, 2 * row, 2 * row - (2 * CHIPS - 1))
+    owner = 2 * ((row + FIRST) & (CHIPS - 1)) + (row >> 6)
     hit = jnp.broadcast_to(target, shape) == owner
     lane_f = lane.astype(jnp.float32)
     first = jnp.min(jnp.where(hit, lane_f, float(TILE_DEV)), axis=1, keepdims=True)
@@ -168,7 +169,10 @@
     inputs = (tension, tile_dest.reshape(1, -1), restriction)
     scratch = [V(x.shape, x.dtype) for x in inputs] + [pltpu.SemaphoreType.DMA((3,))]
     outbox, token = call(pack_kernel, ((CHIPS * ROWS, LANES), (8, LANES)), [pl.ANY] * 3, scratch, 60)(*inputs)
-    inbox = lax.all_to_all(outbox.reshape(CHIPS, ROWS, LANES), "chip", 0, 0, tiled=True)
+    groups = [[2 * ((FIRST + i) % CHIPS) + c for i in range(CHIPS)] for c in range(2)]
+    inbox = lax.all_to_all(
+        outbox.reshape(CHIPS, ROWS, LANES), ("chip", "core"), 0, 0, axis_index_groups=groups, tiled=True
+    )
     index = call(send_index_kernel, (QUAD, SHARED), [V, V, V])(
         elem_block.reshape(-1, LANES), shared_send.reshape(1, -1), token
     )

time: 41.9 us -> 35.5 us (0.85)
  waiting for transfers between devices: 10.4 us -> 4.04 us
  blocking collectives: 4.62 us -> 2.44 us
  starting transfers between devices: 22 us -> 24.1 us
    all_to_all x1, waiting for transfers between devices: 7.51 us -> 1.03 us  [per_device(): lax.all_to_all(outbox.reshape(CHIPS, ROWS, LANES), ('chip', 'core'), 0, 0...]
    all_gather x1, blocking collectives: 4.62 us -> 2.44 us  [per_device(): lax.all_gather(inbox.reshape(CHIPS * ROWS, LANES), 'core', tiled=True)]
    all_to_all x1, starting transfers between devices: 19.1 us -> 21 us  [per_device(): lax.all_to_all(outbox.reshape(CHIPS, ROWS, LANES), ('chip', 'core'), 0, 0...]
where the time goes in v3:
time: 35.5 us; the launch traced here: 35.2 us
  starting transfers between devices  24.1 us (68%)
  waiting for transfers between devices  4.04 us (11%)
  Pallas kernels  3.83 us (11%)
  blocking collectives  2.44 us (7%)
  local copies, waits for them, and re-layouts  0.68 us (2%)
    all_to_all x1, starting transfers between devices, per_device(): lax.all_to_all(outbox.reshape(CHIPS, ROWS, LANES), ('chip', 'core'), 0, 0...  21 us
    ppermute x1, starting transfers between devices, per_device(): lax.ppermute(index, ('chip', 'core'), [(i, (i - 1) % count) for i in rang...  3.14 us
    ppermute x1, waiting for transfers between devices, per_device(): lax.ppermute(index, ('chip', 'core'), [(i, (i - 1) % count) for i in rang...  3 us
    all_gather x1, blocking collectives, per_device(): lax.all_gather(inbox.reshape(CHIPS * ROWS, LANES), 'core', tiled=True)  2.44 us
    pallas_call x1, Pallas kernels, per_device(): call(pack_kernel, ((CHIPS * ROWS, LANES), (8, LANES)), [pl.ANY] * 3, scra...  2.36 us
    pallas_call x1, Pallas kernels, per_device(): call(place_kernel, (QUAD, ELEM_DEV), [S] + [V] * 4)  1.2 us
    all_to_all x1, waiting for transfers between devices, per_device(): lax.all_to_all(outbox.reshape(CHIPS, ROWS, LANES), ('chip', 'core'), 0, 0...  1.03 us
  transfers between devices with their start and end apart: 2, of which 2 were waited for; matrix products, arithmetic and copies ran while one was open for 0% of the time, Pallas kernels for 1%

profile of v3, /device:TPU:1, one launch (start us, length us, event | category | flops | bytes accessed | tf_op | source)
XLA Modules:
  0.0 35.2 jit_solution(6334213584373015937)
XLA Ops:
  0.0 2.4 %pack_kernel.1 = (f32[256,128]{1,0:T(8,128)}, f32[8,128]{1,0:T(8,128)}) custom-call(f32[128,512]{1,0:T(8,128)} %tension_any.1, s32[1,128]{1,0:T(1,128)} %bitcast.18, f32[8,64]{1,0:T(8,128)} %restriction_any.1), custom_call_target="tpu_custom_call" | custom-call | tf_op jit(solution)/shard_map/pack_kernel/pallas_call | solution.py:171
  2.4 0.0 copy-start.1
  2.4 21.0 %all-to-all-start = ((f32[64,4,128]{2,1,0:T(4,128)}), f32[64,4,128]{2,1,0:T(4,128)S(1)}, u32[]{:S(2)}, u32[]{:S(2)}) async-start(f32[64,4,128]{2,1,0:T(4,128)} %bitcast.17), calls=%async_computation | async-start | bytes 262144 | tf_op jit(solution)/shard_map/all_to_all | solution.py:173
  23.4 0.0 copy-start
  23.4 0.0 copy-start.2
  23.4 0.0 copy-done.1
  23.4 0.7 %copy-done = s32[1024]{0:T(1024)S(1)} copy-done((s32[1024]{0:T(1024)S(1)}, s32[1024]{0:T(1024)}, u32[]{:S(2)}) %copy-start) | copy-done | bytes 4120
  24.1 0.0 copy-done.2
  24.1 0.1 send_index_kernel.1
  24.2 3.1 %collective-permute-start = (f32[8,256]{1,0:T(8,128)S(1)}, f32[8,256]{1,0:T(8,128)S(1)}, u32[]{:S(2)}, u32[]{:S(2)}) collective-permute-start(f32[8,256]{1,0:T(8,128)S(1)} %send_index_kernel.1), channel_id=1, source_target_pairs={{0,508},{4,0},{8,4},{12,8},{16,12},{20,16},{24,20},{28,24},{32,28}... | collective-permute-start | bytes 24584 | tf_op jit(solution)/shard_map/ppermute | solution.py:180
  27.4 0.0 copy-start.3
  27.4 3.0 %collective-permute-done.index_ref = f32[8,256]{1,0:T(8,128)S(1)} collective-permute-done((f32[8,256]{1,0:T(8,128)S(1)}, f32[8,256]{1,0:T(8,128)S(1)}, u32[]{:S(2)}, u32[]{:S(2)}) %collective-permute-start) | collective-permute-done | bytes 8224 | tf_op jit(solution)/shard_map/ppermute | solution.py:180
  30.4 0.0 copy-done.3
  30.4 0.1 own_index_kernel.1
  30.5 1.0 %all-to-all-done = f32[64,4,128]{2,1,0:T(4,128)S(1)} async-done(((f32[64,4,128]{2,1,0:T(4,128)}), f32[64,4,128]{2,1,0:T(4,128)S(1)}, u32[]{:S(2)}, u32[]{:S(2)}) %all-to-all-start) | async-done | bytes 131104 | tf_op jit(solution)/shard_map/all_to_all | solution.py:173
  31.6 2.4 %all_gather.3.inbox_ref = f32[512,128]{1,0:T(8,128)S(1)} all-gather(f32[256,128]{1,0:T(8,128)S(1)} %bitcast.16), channel_id=1, replica_groups=mesh['chip'=64,'core'=2,'rep'=4] {'core'}, dimensions={0}, use_global_device_ids=true | all-gather | bytes 393216 | tf_op jit(solution)/shard_map/all_gather | solution.py:182
  34.0 1.2 %place_kernel.1 = f32[8,1024]{1,0:T(8,128)} custom-call(s32[1]{0:T(128)} %bitcast.core_ref, f32[512,128]{1,0:T(8,128)S(1)} %all_gather.3.inbox_ref, s32[1,1024]{1,0:T(1,128)S(1)} %bitcast.11, f32[1,1024]{1,0:T(1,128)S(1)} %bitcast.12, f32[1,1024]{1,0:T(1,128)S(1)} %bitcast.13), custom_call_target="tpu_custom_call" | custom-call | tf_op jit(solution)/shard_map/place_kernel/pallas_call | solution.py:183
Async XLA Ops:
  2.4 21.0 %copy-start.1 = (f32[8,128]{1,0:T(8,128)S(1)}, f32[8,128]{1,0:T(8,128)}, u32[]{:S(2)}) copy-start(f32[8,128]{1,0:T(8,128)} %get-tuple-element.10._) | copy-start | bytes 12292
  2.4 29.2 %all-to-all-start = ((f32[64,4,128]{2,1,0:T(4,128)}), f32[64,4,128]{2,1,0:T(4,128)S(1)}, u32[]{:S(2)}, u32[]{:S(2)}) async-start(f32[64,4,128]{2,1,0:T(4,128)} %bitcast.17), calls=%async_computation | async-start | bytes 262144 | tf_op jit(solution)/shard_map/all_to_all | solution.py:173
  23.4 0.7 %copy-start = (s32[1024]{0:T(1024)S(1)}, s32[1024]{0:T(1024)}, u32[]{:S(2)}) copy-start(s32[1024]{0:T(1024)} %param.9) | copy-start | bytes 12292
  23.4 0.7 %copy-start.2 = (s32[256]{0:T(256)S(1)}, s32[256]{0:T(256)}, u32[]{:S(2)}) copy-start(s32[256]{0:T(256)} %param.11) | copy-start | bytes 3076
  24.2 6.2 %collective-permute-start = (f32[8,256]{1,0:T(8,128)S(1)}, f32[8,256]{1,0:T(8,128)S(1)}, u32[]{:S(2)}, u32[]{:S(2)}) collective-permute-start(f32[8,256]{1,0:T(8,128)S(1)} %send_index_kernel.1), channel_id=1, source_target_pairs={{0,508},{4,0},{8,4},{12,8},{16,12},{20,16},{24,20},{28,24},{32,28}... | collective-permute-start | bytes 24584 | tf_op jit(solution)/shard_map/ppermute | solution.py:180
  27.4 3.0 %copy-start.3 = (s32[256]{0:T(256)S(1)}, s32[256]{0:T(256)}, u32[]{:S(2)}) copy-start(s32[256]{0:T(256)} %param.10) | copy-start | bytes 3076

commit v4 on v3

--- a/solution.py
+++ b/solution.py
@@ -16,6 +16,7 @@
 CHIPS = 64
 ROWS = 4
 FIRST = 42
+RING = 16
 
 
 def iota(shape, dim):
@@ -169,7 +170,8 @@
     inputs = (tension, tile_dest.reshape(1, -1), restriction)
     scratch = [V(x.shape, x.dtype) for x in inputs] + [pltpu.SemaphoreType.DMA((3,))]
     outbox, token = call(pack_kernel, ((CHIPS * ROWS, LANES), (8, LANES)), [pl.ANY] * 3, scratch, 60)(*inputs)
-    groups = [[2 * ((FIRST + i) % CHIPS) + c for i in range(CHIPS)] for c in range(2)]
+    order = [(FIRST + i) % CHIPS for i in range(CHIPS)]
+    groups = [[2 * chip + (c ^ (chip % RING == 0)) for chip in order] for c in range(2)]
     inbox = lax.all_to_all(
         outbox.reshape(CHIPS, ROWS, LANES), ("chip", "core"), 0, 0, axis_index_groups=groups, tiled=True
     )

time: 35.5 us -> 35.2 us (level)
  waiting for transfers between devices: 4.04 us -> 4.57 us
  blocking collectives: 2.44 us -> 2.03 us
  starting transfers between devices: 24.1 us -> 23.7 us
    ppermute x1, starting transfers between devices: 3.14 us -> 1.92 us  [per_device(): lax.ppermute(index, ('chip', 'core'), [(i, (i - 1) % count) for i in rang...]
    all_to_all x1, starting transfers between devices: 21 us -> 21.8 us  [per_device(): lax.all_to_all(outbox.reshape(CHIPS, ROWS, LANES), ('chip', 'core'), 0, 0...]
    ppermute x1, waiting for transfers between devices: 3 us -> 3.47 us  [per_device(): lax.ppermute(index, ('chip', 'core'), [(i, (i - 1) % count) for i in rang...]
    all_gather x1, blocking collectives: 2.44 us -> 2.03 us  [per_device(): lax.all_gather(inbox.reshape(CHIPS * ROWS, LANES), 'core', tiled=True)]
where the time goes in v4:
time: 35.2 us; the launch traced here: 34.9 us
  starting transfers between devices  23.7 us (67%)
  waiting for transfers between devices  4.57 us (13%)
  Pallas kernels  3.83 us (11%)
  blocking collectives  2.03 us (6%)
  local copies, waits for them, and re-layouts  0.68 us (2%)
    all_to_all x1, starting transfers between devices, per_device(): lax.all_to_all(outbox.reshape(CHIPS, ROWS, LANES), ('chip', 'core'), 0, 0...  21.8 us
    ppermute x1, waiting for transfers between devices, per_device(): lax.ppermute(index, ('chip', 'core'), [(i, (i - 1) % count) for i in rang...  3.47 us
    pallas_call x1, Pallas kernels, per_device(): call(pack_kernel, ((CHIPS * ROWS, LANES), (8, LANES)), [pl.ANY] * 3, scra...  2.36 us
    all_gather x1, blocking collectives, per_device(): lax.all_gather(inbox.reshape(CHIPS * ROWS, LANES), 'core', tiled=True)  2.03 us
    ppermute x1, starting transfers between devices, per_device(): lax.ppermute(index, ('chip', 'core'), [(i, (i - 1) % count) for i in rang...  1.92 us
    pallas_call x1, Pallas kernels, per_device(): call(place_kernel, (QUAD, ELEM_DEV), [S] + [V] * 4)  1.2 us
    all_to_all x1, waiting for transfers between devices, per_device(): lax.all_to_all(outbox.reshape(CHIPS, ROWS, LANES), ('chip', 'core'), 0, 0...  1.1 us
  transfers between devices with their start and end apart: 2, of which 2 were waited for; matrix products, arithmetic and copies ran while one was open for 0% of the time, Pallas kernels for 1%

profile of v4, /device:TPU:1, one launch (start us, length us, event | category | flops | bytes accessed | tf_op | source)
XLA Modules:
  0.0 34.9 jit_solution(3352695412015181764)
XLA Ops:
  0.0 2.4 %pack_kernel.1 = (f32[256,128]{1,0:T(8,128)}, f32[8,128]{1,0:T(8,128)}) custom-call(f32[128,512]{1,0:T(8,128)} %tension_any.1, s32[1,128]{1,0:T(1,128)} %bitcast.18, f32[8,64]{1,0:T(8,128)} %restriction_any.1), custom_call_target="tpu_custom_call" | custom-call | tf_op jit(solution)/shard_map/pack_kernel/pallas_call | solution.py:172
  2.4 0.0 copy-start.1
  2.4 21.8 %all-to-all-start = ((f32[64,4,128]{2,1,0:T(4,128)}), f32[64,4,128]{2,1,0:T(4,128)S(1)}, u32[]{:S(2)}, u32[]{:S(2)}) async-start(f32[64,4,128]{2,1,0:T(4,128)} %bitcast.17), calls=%async_computation | async-start | bytes 262144 | tf_op jit(solution)/shard_map/all_to_all | solution.py:175
  24.2 0.0 copy-start
  24.2 0.0 copy-start.2
  24.2 0.0 copy-done.1
  24.3 0.7 %copy-done = s32[1024]{0:T(1024)S(1)} copy-done((s32[1024]{0:T(1024)S(1)}, s32[1024]{0:T(1024)}, u32[]{:S(2)}) %copy-start) | copy-done | bytes 4120
  24.9 0.0 copy-done.2
  24.9 0.1 send_index_kernel.1
  25.1 1.9 %collective-permute-start = (f32[8,256]{1,0:T(8,128)S(1)}, f32[8,256]{1,0:T(8,128)S(1)}, u32[]{:S(2)}, u32[]{:S(2)}) collective-permute-start(f32[8,256]{1,0:T(8,128)S(1)} %send_index_kernel.1), channel_id=1, source_target_pairs={{0,508},{4,0},{8,4},{12,8},{16,12},{20,16},{24,20},{28,24},{32,28}... | collective-permute-start | bytes 24584 | tf_op jit(solution)/shard_map/ppermute | solution.py:182
  27.0 0.0 copy-start.3
  27.0 3.5 %collective-permute-done.index_ref = f32[8,256]{1,0:T(8,128)S(1)} collective-permute-done((f32[8,256]{1,0:T(8,128)S(1)}, f32[8,256]{1,0:T(8,128)S(1)}, u32[]{:S(2)}, u32[]{:S(2)}) %collective-permute-start) | collective-permute-done | bytes 8224 | tf_op jit(solution)/shard_map/ppermute | solution.py:182
  30.5 0.0 copy-done.3
  30.5 0.1 own_index_kernel.1
  30.6 1.1 %all-to-all-done = f32[64,4,128]{2,1,0:T(4,128)S(1)} async-done(((f32[64,4,128]{2,1,0:T(4,128)}), f32[64,4,128]{2,1,0:T(4,128)S(1)}, u32[]{:S(2)}, u32[]{:S(2)}) %all-to-all-start) | async-done | bytes 131104 | tf_op jit(solution)/shard_map/all_to_all | solution.py:175
  31.7 2.0 %all_gather.3.inbox_ref = f32[512,128]{1,0:T(8,128)S(1)} all-gather(f32[256,128]{1,0:T(8,128)S(1)} %bitcast.16), channel_id=1, replica_groups=mesh['chip'=64,'core'=2,'rep'=4] {'core'}, dimensions={0}, use_global_device_ids=true | all-gather | bytes 393216 | tf_op jit(solution)/shard_map/all_gather | solution.py:184
  33.8 1.2 %place_kernel.1 = f32[8,1024]{1,0:T(8,128)} custom-call(s32[1]{0:T(128)} %bitcast.core_ref, f32[512,128]{1,0:T(8,128)S(1)} %all_gather.3.inbox_ref, s32[1,1024]{1,0:T(1,128)S(1)} %bitcast.11, f32[1,1024]{1,0:T(1,128)S(1)} %bitcast.12, f32[1,1024]{1,0:T(1,128)S(1)} %bitcast.13), custom_call_target="tpu_custom_call" | custom-call | tf_op jit(solution)/shard_map/place_kernel/pallas_call | solution.py:185
Async XLA Ops:
  2.4 21.9 %copy-start.1 = (f32[8,128]{1,0:T(8,128)S(1)}, f32[8,128]{1,0:T(8,128)}, u32[]{:S(2)}) copy-start(f32[8,128]{1,0:T(8,128)} %get-tuple-element.10._) | copy-start | bytes 12292
  2.4 29.3 %all-to-all-start = ((f32[64,4,128]{2,1,0:T(4,128)}), f32[64,4,128]{2,1,0:T(4,128)S(1)}, u32[]{:S(2)}, u32[]{:S(2)}) async-start(f32[64,4,128]{2,1,0:T(4,128)} %bitcast.17), calls=%async_computation | async-start | bytes 262144 | tf_op jit(solution)/shard_map/all_to_all | solution.py:175
  24.2 0.7 %copy-start = (s32[1024]{0:T(1024)S(1)}, s32[1024]{0:T(1024)}, u32[]{:S(2)}) copy-start(s32[1024]{0:T(1024)} %param.9) | copy-start | bytes 12292
  24.2 0.7 %copy-start.2 = (s32[256]{0:T(256)S(1)}, s32[256]{0:T(256)}, u32[]{:S(2)}) copy-start(s32[256]{0:T(256)} %param.11) | copy-start | bytes 3076
  25.1 5.4 %collective-permute-start = (f32[8,256]{1,0:T(8,128)S(1)}, f32[8,256]{1,0:T(8,128)S(1)}, u32[]{:S(2)}, u32[]{:S(2)}) collective-permute-start(f32[8,256]{1,0:T(8,128)S(1)} %send_index_kernel.1), channel_id=1, source_target_pairs={{0,508},{4,0},{8,4},{12,8},{16,12},{20,16},{24,20},{28,24},{32,28}... | collective-permute-start | bytes 24584 | tf_op jit(solution)/shard_map/ppermute | solution.py:182
  27.0 3.5 %copy-start.3 = (s32[256]{0:T(256)S(1)}, s32[256]{0:T(256)}, u32[]{:S(2)}) copy-start(s32[256]{0:T(256)} %param.10) | copy-start | bytes 3076

commit v5 on v4

--- a/solution.py
+++ b/solution.py
@@ -17,6 +17,7 @@
 ROWS = 4
 FIRST = 42
 RING = 16
+STRIDE = 3
 
 
 def iota(shape, dim):
@@ -50,7 +51,7 @@
     position = (dest & (TILE_DEV - 1)).astype(jnp.float32)
     shape = (2 * CHIPS, TILE_DEV)
     row, lane = iota(shape, 0), iota(shape, 1)
-    owner = 2 * ((row + FIRST) & (CHIPS - 1)) + (row >> 6)
+    owner = 2 * ((STRIDE * row + FIRST) & (CHIPS - 1)) + (row >> 6)
     hit = jnp.broadcast_to(target, shape) == owner
     lane_f = lane.astype(jnp.float32)
     first = jnp.min(jnp.where(hit, lane_f, float(TILE_DEV)), axis=1, keepdims=True)
@@ -74,7 +75,8 @@
     even, odd = data[:CHIPS], data[CHIPS:]
 
     def ahead(x):
-        return jnp.concatenate([x[1:], x[:1]], axis=0)
+        step = pow(STRIDE, -1, CHIPS)
+        return jnp.concatenate([x[step:], x[:step]], axis=0)
 
     column = lane[:CHIPS]
     places = jnp.zeros((CHIPS, LANES), jnp.float32)
@@ -170,7 +172,7 @@
     inputs = (tension, tile_dest.reshape(1, -1), restriction)
     scratch = [V(x.shape, x.dtype) for x in inputs] + [pltpu.SemaphoreType.DMA((3,))]
     outbox, token = call(pack_kernel, ((CHIPS * ROWS, LANES), (8, LANES)), [pl.ANY] * 3, scratch, 60)(*inputs)
-    order = [(FIRST + i) % CHIPS for i in range(CHIPS)]
+    order = [(FIRST + STRIDE * i) % CHIPS for i in range(CHIPS)]
     groups = [[2 * chip + (c ^ (chip % RING == 0)) for chip in order] for c in range(2)]
     inbox = lax.all_to_all(
         outbox.reshape(CHIPS, ROWS, LANES), ("chip", "core"), 0, 0, axis_index_groups=groups, tiled=True

time: 35.2 us -> 35 us (level)
    all_to_all x1, waiting for transfers between devices: 1.1 us -> 0.72 us  [per_device(): lax.all_to_all(outbox.reshape(CHIPS, ROWS, LANES), ('chip', 'core'), 0, 0...]
where the time goes in v5:
time: 35 us; the launch traced here: 34.8 us
  starting transfers between devices  23.9 us (68%)
  waiting for transfers between devices  4.23 us (12%)
  Pallas kernels  3.83 us (11%)
  blocking collectives  2 us (6%)
  local copies, waits for them, and re-layouts  0.68 us (2%)
    all_to_all x1, starting transfers between devices, per_device(): lax.all_to_all(outbox.reshape(CHIPS, ROWS, LANES), ('chip', 'core'), 0, 0...  22 us
    ppermute x1, waiting for transfers between devices, per_device(): lax.ppermute(index, ('chip', 'core'), [(i, (i - 1) % count) for i in rang...  3.51 us
    pallas_call x1, Pallas kernels, per_device(): call(pack_kernel, ((CHIPS * ROWS, LANES), (8, LANES)), [pl.ANY] * 3, scra...  2.36 us
    all_gather x1, blocking collectives, per_device(): lax.all_gather(inbox.reshape(CHIPS * ROWS, LANES), 'core', tiled=True)  2 us
    ppermute x1, starting transfers between devices, per_device(): lax.ppermute(index, ('chip', 'core'), [(i, (i - 1) % count) for i in rang...  1.92 us
    pallas_call x1, Pallas kernels, per_device(): call(place_kernel, (QUAD, ELEM_DEV), [S] + [V] * 4)  1.19 us
    all_to_all x1, waiting for transfers between devices, per_device(): lax.all_to_all(outbox.reshape(CHIPS, ROWS, LANES), ('chip', 'core'), 0, 0...  0.72 us
  transfers between devices with their start and end apart: 2, of which 2 were waited for; matrix products, arithmetic and copies ran while one was open for 0% of the time, Pallas kernels for 1%

profile of v5, /device:TPU:1, one launch (start us, length us, event | category | flops | bytes accessed | tf_op | source)
XLA Modules:
  0.0 34.8 jit_solution(2172393870701590023)
XLA Ops:
  0.0 2.4 %pack_kernel.1 = (f32[256,128]{1,0:T(8,128)}, f32[8,128]{1,0:T(8,128)}) custom-call(f32[128,512]{1,0:T(8,128)} %tension_any.1, s32[1,128]{1,0:T(1,128)} %bitcast.18, f32[8,64]{1,0:T(8,128)} %restriction_any.1), custom_call_target="tpu_custom_call" | custom-call | tf_op jit(solution)/shard_map/pack_kernel/pallas_call | solution.py:174
  2.4 0.0 copy-start.1
  2.4 22.0 %all-to-all-start = ((f32[64,4,128]{2,1,0:T(4,128)}), f32[64,4,128]{2,1,0:T(4,128)S(1)}, u32[]{:S(2)}, u32[]{:S(2)}) async-start(f32[64,4,128]{2,1,0:T(4,128)} %bitcast.17), calls=%async_computation | async-start | bytes 262144 | tf_op jit(solution)/shard_map/all_to_all | solution.py:177
  24.4 0.0 copy-start
  24.4 0.0 copy-start.2
  24.4 0.0 copy-done.1
  24.4 0.7 %copy-done = s32[1024]{0:T(1024)S(1)} copy-done((s32[1024]{0:T(1024)S(1)}, s32[1024]{0:T(1024)}, u32[]{:S(2)}) %copy-start) | copy-done | bytes 4120
  25.1 0.0 copy-done.2
  25.1 0.1 send_index_kernel.1
  25.3 1.9 %collective-permute-start = (f32[8,256]{1,0:T(8,128)S(1)}, f32[8,256]{1,0:T(8,128)S(1)}, u32[]{:S(2)}, u32[]{:S(2)}) collective-permute-start(f32[8,256]{1,0:T(8,128)S(1)} %send_index_kernel.1), channel_id=1, source_target_pairs={{0,508},{4,0},{8,4},{12,8},{16,12},{20,16},{24,20},{28,24},{32,28}... | collective-permute-start | bytes 24584 | tf_op jit(solution)/shard_map/ppermute | solution.py:184
  27.2 0.0 copy-start.3
  27.2 3.5 %collective-permute-done.index_ref = f32[8,256]{1,0:T(8,128)S(1)} collective-permute-done((f32[8,256]{1,0:T(8,128)S(1)}, f32[8,256]{1,0:T(8,128)S(1)}, u32[]{:S(2)}, u32[]{:S(2)}) %collective-permute-start) | collective-permute-done | bytes 8224 | tf_op jit(solution)/shard_map/ppermute | solution.py:184
  30.7 0.0 copy-done.3
  30.7 0.1 own_index_kernel.1
  30.8 0.7 %all-to-all-done = f32[64,4,128]{2,1,0:T(4,128)S(1)} async-done(((f32[64,4,128]{2,1,0:T(4,128)}), f32[64,4,128]{2,1,0:T(4,128)S(1)}, u32[]{:S(2)}, u32[]{:S(2)}) %all-to-all-start) | async-done | bytes 131104 | tf_op jit(solution)/shard_map/all_to_all | solution.py:177
  31.6 2.0 %all_gather.3.inbox_ref = f32[512,128]{1,0:T(8,128)S(1)} all-gather(f32[256,128]{1,0:T(8,128)S(1)} %bitcast.16), channel_id=1, replica_groups=mesh['chip'=64,'core'=2,'rep'=4] {'core'}, dimensions={0}, use_global_device_ids=true | all-gather | bytes 393216 | tf_op jit(solution)/shard_map/all_gather | solution.py:186
  33.6 1.2 %place_kernel.1 = f32[8,1024]{1,0:T(8,128)} custom-call(s32[1]{0:T(128)} %bitcast.core_ref, f32[512,128]{1,0:T(8,128)S(1)} %all_gather.3.inbox_ref, s32[1,1024]{1,0:T(1,128)S(1)} %bitcast.11, f32[1,1024]{1,0:T(1,128)S(1)} %bitcast.12, f32[1,1024]{1,0:T(1,128)S(1)} %bitcast.13), custom_call_target="tpu_custom_call" | custom-call | tf_op jit(solution)/shard_map/place_kernel/pallas_call | solution.py:187
Async XLA Ops:
  2.4 22.1 %copy-start.1 = (f32[8,128]{1,0:T(8,128)S(1)}, f32[8,128]{1,0:T(8,128)}, u32[]{:S(2)}) copy-start(f32[8,128]{1,0:T(8,128)} %get-tuple-element.10._) | copy-start | bytes 12292
  2.4 29.2 %all-to-all-start = ((f32[64,4,128]{2,1,0:T(4,128)}), f32[64,4,128]{2,1,0:T(4,128)S(1)}, u32[]{:S(2)}, u32[]{:S(2)}) async-start(f32[64,4,128]{2,1,0:T(4,128)} %bitcast.17), calls=%async_computation | async-start | bytes 262144 | tf_op jit(solution)/shard_map/all_to_all | solution.py:177
  24.4 0.7 %copy-start = (s32[1024]{0:T(1024)S(1)}, s32[1024]{0:T(1024)}, u32[]{:S(2)}) copy-start(s32[1024]{0:T(1024)} %param.9) | copy-start | bytes 12292
  24.4 0.7 %copy-start.2 = (s32[256]{0:T(256)S(1)}, s32[256]{0:T(256)}, u32[]{:S(2)}) copy-start(s32[256]{0:T(256)} %param.11) | copy-start | bytes 3076
  25.3 5.5 %collective-permute-start = (f32[8,256]{1,0:T(8,128)S(1)}, f32[8,256]{1,0:T(8,128)S(1)}, u32[]{:S(2)}, u32[]{:S(2)}) collective-permute-start(f32[8,256]{1,0:T(8,128)S(1)} %send_index_kernel.1), channel_id=1, source_target_pairs={{0,508},{4,0},{8,4},{12,8},{16,12},{20,16},{24,20},{28,24},{32,28}... | collective-permute-start | bytes 24584 | tf_op jit(solution)/shard_map/ppermute | solution.py:184
  27.2 3.5 %copy-start.3 = (s32[256]{0:T(256)S(1)}, s32[256]{0:T(256)}, u32[]{:S(2)}) copy-start(s32[256]{0:T(256)} %param.10) | copy-start | bytes 3076

commit v6 on v5

--- a/solution.py
+++ b/solution.py
@@ -123,9 +123,10 @@
         [jnp.concatenate([part[:WIDTH], part[WIDTH:]], axis=1) for part in split3(turned)], axis=0
     )
     shape = (TILE_DEV, tile.shape[1])
-    wide = jnp.broadcast_to(tile, shape)
+    wide = jnp.broadcast_to(tile.astype(jnp.bfloat16), shape)
+    one, nil = jnp.ones(shape, jnp.bfloat16), jnp.zeros(shape, jnp.bfloat16)
     pick = jnp.concatenate(
-        [jnp.where(jnp.broadcast_to(place, shape) == wide, 1.0, 0.0).astype(jnp.bfloat16) for place in places], axis=0
+        [jnp.where(jnp.concatenate([jnp.broadcast_to(place, (TILE_DEV, LANES)).astype(jnp.bfloat16)] * (shape[1] // LANES), axis=1) == wide, one, nil) for place in places], axis=0
     )
     tall = dot(left, pick, (1, 0))
     tall = tall[:WIDTH] + tall[WIDTH : 2 * WIDTH] + tall[2 * WIDTH :]

time: 35 us -> 35 us (level)
  no operation moved by 1% of the time
where the time goes in v6:
time: 35 us; the launch traced here: 34.7 us
  starting transfers between devices  23.9 us (68%)
  waiting for transfers between devices  4.23 us (12%)
  Pallas kernels  3.79 us (11%)
  blocking collectives  2 us (6%)
  local copies, waits for them, and re-layouts  0.68 us (2%)
    all_to_all x1, starting transfers between devices, per_device(): lax.all_to_all(outbox.reshape(CHIPS, ROWS, LANES), ('chip', 'core'), 0, 0...  22 us
    ppermute x1, waiting for transfers between devices, per_device(): lax.ppermute(index, ('chip', 'core'), [(i, (i - 1) % count) for i in rang...  3.51 us
    pallas_call x1, Pallas kernels, per_device(): call(pack_kernel, ((CHIPS * ROWS, LANES), (8, LANES)), [pl.ANY] * 3, scra...  2.36 us
    all_gather x1, blocking collectives, per_device(): lax.all_gather(inbox.reshape(CHIPS * ROWS, LANES), 'core', tiled=True)  2 us
    ppermute x1, starting transfers between devices, per_device(): lax.ppermute(index, ('chip', 'core'), [(i, (i - 1) % count) for i in rang...  1.92 us
    pallas_call x1, Pallas kernels, per_device(): call(place_kernel, (QUAD, ELEM_DEV), [S] + [V] * 4)  1.16 us
    all_to_all x1, waiting for transfers between devices, per_device(): lax.all_to_all(outbox.reshape(CHIPS, ROWS, LANES), ('chip', 'core'), 0, 0...  0.72 us
  transfers between devices with their start and end apart: 2, of which 2 were waited for; matrix products, arithmetic and copies ran while one was open for 0% of the time, Pallas kernels for 1%

profile of v6, /device:TPU:1, one launch (start us, length us, event | category | flops | bytes accessed | tf_op | source)
XLA Modules:
  0.0 34.7 jit_solution(13020434689506228625)
XLA Ops:
  0.0 2.4 %pack_kernel.1 = (f32[256,128]{1,0:T(8,128)}, f32[8,128]{1,0:T(8,128)}) custom-call(f32[128,512]{1,0:T(8,128)} %tension_any.1, s32[1,128]{1,0:T(1,128)} %bitcast.18, f32[8,64]{1,0:T(8,128)} %restriction_any.1), custom_call_target="tpu_custom_call" | custom-call | tf_op jit(solution)/shard_map/pack_kernel/pallas_call | solution.py:175
  2.4 0.0 copy-start.1
  2.4 22.0 %all-to-all-start = ((f32[64,4,128]{2,1,0:T(4,128)}), f32[64,4,128]{2,1,0:T(4,128)S(1)}, u32[]{:S(2)}, u32[]{:S(2)}) async-start(f32[64,4,128]{2,1,0:T(4,128)} %bitcast.17), calls=%async_computation | async-start | bytes 262144 | tf_op jit(solution)/shard_map/all_to_all | solution.py:178
  24.4 0.0 copy-start
  24.4 0.0 copy-start.2
  24.4 0.0 copy-done.1
  24.4 0.7 %copy-done = s32[1024]{0:T(1024)S(1)} copy-done((s32[1024]{0:T(1024)S(1)}, s32[1024]{0:T(1024)}, u32[]{:S(2)}) %copy-start) | copy-done | bytes 4120
  25.1 0.0 copy-done.2
  25.1 0.1 send_index_kernel.1
  25.3 1.9 %collective-permute-start = (f32[8,256]{1,0:T(8,128)S(1)}, f32[8,256]{1,0:T(8,128)S(1)}, u32[]{:S(2)}, u32[]{:S(2)}) collective-permute-start(f32[8,256]{1,0:T(8,128)S(1)} %send_index_kernel.1), channel_id=1, source_target_pairs={{0,508},{4,0},{8,4},{12,8},{16,12},{20,16},{24,20},{28,24},{32,28}... | collective-permute-start | bytes 24584 | tf_op jit(solution)/shard_map/ppermute | solution.py:185
  27.2 0.0 copy-start.3
  27.2 3.5 %collective-permute-done.index_ref = f32[8,256]{1,0:T(8,128)S(1)} collective-permute-done((f32[8,256]{1,0:T(8,128)S(1)}, f32[8,256]{1,0:T(8,128)S(1)}, u32[]{:S(2)}, u32[]{:S(2)}) %collective-permute-start) | collective-permute-done | bytes 8224 | tf_op jit(solution)/shard_map/ppermute | solution.py:185
  30.7 0.0 copy-done.3
  30.7 0.1 own_index_kernel.1
  30.8 0.7 %all-to-all-done = f32[64,4,128]{2,1,0:T(4,128)S(1)} async-done(((f32[64,4,128]{2,1,0:T(4,128)}), f32[64,4,128]{2,1,0:T(4,128)S(1)}, u32[]{:S(2)}, u32[]{:S(2)}) %all-to-all-start) | async-done | bytes 131104 | tf_op jit(solution)/shard_map/all_to_all | solution.py:178
  31.6 2.0 %all_gather.3.inbox_ref = f32[512,128]{1,0:T(8,128)S(1)} all-gather(f32[256,128]{1,0:T(8,128)S(1)} %bitcast.16), channel_id=1, replica_groups=mesh['chip'=64,'core'=2,'rep'=4] {'core'}, dimensions={0}, use_global_device_ids=true | all-gather | bytes 393216 | tf_op jit(solution)/shard_map/all_gather | solution.py:187
  33.6 1.2 %place_kernel.1 = f32[8,1024]{1,0:T(8,128)} custom-call(s32[1]{0:T(128)} %bitcast.core_ref, f32[512,128]{1,0:T(8,128)S(1)} %all_gather.3.inbox_ref, s32[1,1024]{1,0:T(1,128)S(1)} %bitcast.11, f32[1,1024]{1,0:T(1,128)S(1)} %bitcast.12, f32[1,1024]{1,0:T(1,128)S(1)} %bitcast.13), custom_call_target="tpu_custom_call" | custom-call | tf_op jit(solution)/shard_map/place_kernel/pallas_call | solution.py:188
Async XLA Ops:
  2.4 22.1 %copy-start.1 = (f32[8,128]{1,0:T(8,128)S(1)}, f32[8,128]{1,0:T(8,128)}, u32[]{:S(2)}) copy-start(f32[8,128]{1,0:T(8,128)} %get-tuple-element.10._) | copy-start | bytes 12292
  2.4 29.2 %all-to-all-start = ((f32[64,4,128]{2,1,0:T(4,128)}), f32[64,4,128]{2,1,0:T(4,128)S(1)}, u32[]{:S(2)}, u32[]{:S(2)}) async-start(f32[64,4,128]{2,1,0:T(4,128)} %bitcast.17), calls=%async_computation | async-start | bytes 262144 | tf_op jit(solution)/shard_map/all_to_all | solution.py:178
  24.4 0.7 %copy-start = (s32[1024]{0:T(1024)S(1)}, s32[1024]{0:T(1024)}, u32[]{:S(2)}) copy-start(s32[1024]{0:T(1024)} %param.9) | copy-start | bytes 12292
  24.4 0.7 %copy-start.2 = (s32[256]{0:T(256)S(1)}, s32[256]{0:T(256)}, u32[]{:S(2)}) copy-start(s32[256]{0:T(256)} %param.11) | copy-start | bytes 3076
  25.3 5.5 %collective-permute-start = (f32[8,256]{1,0:T(8,128)S(1)}, f32[8,256]{1,0:T(8,128)S(1)}, u32[]{:S(2)}, u32[]{:S(2)}) collective-permute-start(f32[8,256]{1,0:T(8,128)S(1)} %send_index_kernel.1), channel_id=1, source_target_pairs={{0,508},{4,0},{8,4},{12,8},{16,12},{20,16},{24,20},{28,24},{32,28}... | collective-permute-start | bytes 24584 | tf_op jit(solution)/shard_map/ppermute | solution.py:185
  27.2 3.5 %copy-start.3 = (s32[256]{0:T(256)S(1)}, s32[256]{0:T(256)}, u32[]{:S(2)}) copy-start(s32[256]{0:T(256)} %param.10) | copy-start | bytes 3076
